TPU v7x, 512 devices: a 8x2x16 block of a 8x16x16 slice. The times are simulated.
512 devices in a mesh: groups: 2 (over y), seq: 16 (over z), side: 2 (over core), req: 8 (over x).
Axes of the slice: x: 8, y: 2, z: 16, core: 2. Of those that a mesh axis runs over, the one named last changes fastest.
The devices are a block of a 8x16x16 slice.
Arguments:
- queries: bfloat16 [16, 128, 4, 2048], P(('groups', 'req'), 'seq', 'side'), parts along dimension 0, may hold values from -8 to 8
- cache_keys: bfloat16 [16, 2048, 512], P(('groups', 'req'), 'seq', 'side'), parts along dimension 0, may hold values from -8 to 8
- cache_values: bfloat16 [16, 2048, 512], P(('groups', 'req'), 'seq', 'side'), parts along dimension 0, may hold values from -6 to 6
- tree_keys: bfloat16 [16, 128, 512], P(('groups', 'req'), 'seq', 'side'), parts along dimension 0, may hold values from -8 to 8
- tree_values: bfloat16 [16, 128, 512], P(('groups', 'req'), 'seq', 'side'), parts along dimension 0, may hold values from -6 to 6
- parents: int32 [16, 128], P(('groups', 'req')), parts along dimension 0, may hold values from 0 to 126, as said below
- lengths: int32 [16], P(('groups', 'req')), parts along dimension 0, may hold values from 256 to 2048
- out_weight: bfloat16 [4, 2048, 4096], P('side', 'seq', 'req'), may hold values from -0.0625 to 0.0625
- in_experts: bfloat16 [64, 4096, 1024], P(('seq', 'side'), 'req'), may hold values from -0.09375 to 0.09375
- out_experts: bfloat16 [64, 1024, 4096], P(('seq', 'side'), None, 'req'), may hold values from -0.1875 to 0.1875
- gate_experts: int32 [2048, 8], P(('groups', 'seq', 'side')), parts along dimension 0, may hold values from 0 to 63, all different within a row; in each aligned block of 32 rows (0 to 31, 32 to 63, ...) at most 6 rows name the same one
- gate_weights: float32 [2048, 8], P(('groups', 'seq', 'side')), parts along dimension 0, may hold values from 0.1 to 1
Outputs:
- attended: bfloat16 [2048, 4096], P(('groups', 'seq', 'side'), 'req'), parts along dimension 0
- expert_out: bfloat16 [2048, 4096], P(('groups', 'seq', 'side'), 'req'), parts along dimension 0
There are 2 independent parts, one for each index of `groups`. A program takes and returns all parts, laid end to end along the dimension named above; an argument that names none is the same for every part. Nothing has to cross between parts.
Inputs may be any that keep to these rules, and one draw needn't show every extreme that they name: parents[r, 0] is 0; every node i >= 1 has its parent among nodes i - 4 to i - 1. `gate_experts`: within the 32 rows that one device holds along seq+side, no expert is named by more than 6 rows, and in some such block one expert is named exactly 6 times.
All inputs are finite; a program needn't handle non-finite values.
Results may differ from a plain program's by a relative error of at most 0.018.
Values may be sent and summed in bfloat16 or wider, within the bound.
A program may use at most 128 MiB of HBM per device.

v0:
```python
import math

import jax
import jax.numpy as jnp
from jax import lax
from jax.sharding import PartitionSpec as P

GROUP = 16
HD = 128
EXPERTS = 64
CAP = 6


NEG_FILL = -1e30


def joined_along(blocks, dim):
    blocks = jnp.moveaxis(blocks, 0, dim)
    lengths = blocks.shape
    return blocks.reshape(*lengths[:dim], lengths[dim] * lengths[dim + 1], *lengths[dim + 2 :])


def sent_to_all(x, axis):
    copies = jnp.broadcast_to(x, (lax.axis_size(axis), *x.shape))
    return lax.all_to_all(copies, axis, split_axis=0, concat_axis=0, tiled=True)


def collect(x, axis, dim):
    return joined_along(sent_to_all(x, axis), dim)


def sent_together(arrays, axis, split_dim, concat_dim, along):
    columns = [a.reshape(*a.shape[:along], -1) for a in arrays]
    both = jnp.concatenate(columns, axis=along)
    filled, at, gathered = (
        lax.all_to_all(both, axis, split_axis=split_dim, concat_axis=concat_dim, tiled=True),
        0,
        [],
    )
    for a, column in zip(arrays, columns):
        slab = filled[..., at : at + column.shape[along]]
        gathered.append(slab.reshape(*slab.shape[:along], *a.shape[along:]))
        at += column.shape[along]
    return tuple(gathered)


def in_blocks(x, dim, count):
    before, after = (x.shape[:dim], x.shape[dim + 1 :])
    return jnp.moveaxis(x.reshape(*before, count, -1, *after), dim, 0)


def sum_at_owner(x, axis, dim):
    count = lax.axis_size(axis)
    blocks = lax.all_to_all(in_blocks(x, dim, count), axis, 0, 0, tiled=True)
    return jnp.sum(blocks, axis=0)


def ancestors(parent_row, node_count):
    node_ids = jnp.arange(node_count, dtype=jnp.int32)
    parent_hit = (node_ids[None, :] == parent_row[:, None]).astype(jnp.float32)
    reached = jnp.maximum(parent_hit, jnp.eye(node_count, dtype=jnp.float32))
    for turn_number in range(max(1, (node_count - 1).bit_length())):
        reached = jnp.minimum(jnp.dot(reached, reached, precision=lax.Precision.HIGHEST), 1.0)
    return reached


def per_device(
    queries,
    cache_keys,
    cache_values,
    tree_keys,
    tree_values,
    parents,
    lengths,
    out_weight,
    in_experts,
    out_experts,
    gate_experts,
    gate_weights,
):
    seq_index = lax.axis_index("seq")
    ctx_local = cache_keys.shape[1]
    nodes_local = queries.shape[1]
    kv_local = queries.shape[2]
    gathered = collect(queries, "seq", 1)
    node_count = gathered.shape[1]
    reached = ancestors(parents[0], node_count)
    tree_seen = lax.dynamic_slice_in_dim(reached, seq_index * nodes_local, nodes_local, 1) > 0.5
    positions = seq_index * ctx_local + jnp.arange(ctx_local, dtype=jnp.int32)
    context_seen = jnp.broadcast_to((positions < lengths[0])[None, :], (node_count, ctx_local))
    visible = jnp.concatenate([context_seen, tree_seen], axis=1)[None]
    factor = 1.0 / math.sqrt(HD)
    outputs, maxima, totals = ([], [], [])
    for head_pair in range(kv_local):
        first_col = head_pair * HD
        key_rows = jnp.concatenate(
            [
                cache_keys[0, :, first_col : first_col + HD],
                tree_keys[0, :, first_col : first_col + HD],
            ],
            axis=0,
        )
        value_rows = jnp.concatenate(
            [
                cache_values[0, :, first_col : first_col + HD],
                tree_values[0, :, first_col : first_col + HD],
            ],
            axis=0,
        )
        query_block = gathered[0, :, head_pair].reshape(node_count, GROUP, HD)
        scores = (
            jnp.einsum("ngd,kd->gnk", query_block, key_rows, preferred_element_type=jnp.float32)
            * factor
        )
        masked = jnp.where(visible, scores, NEG_FILL)
        row_max = jnp.max(masked, axis=-1)
        weights = jnp.where(visible, jnp.exp(masked - row_max[..., None]), 0.0)
        weights_low = weights.astype(jnp.bfloat16)
        outputs.append(
            jnp.einsum("gnk,kd->gnd", weights_low, value_rows, preferred_element_type=jnp.float32)
        )
        maxima.append(row_max)
        totals.append(jnp.sum(weights, axis=-1))
    partial_out = jnp.stack(outputs)
    partial_max = jnp.stack(maxima)
    partial_sum = jnp.stack(totals)
    pieces = sent_together(
        (partial_out[None], partial_max[None], partial_sum[None]), "seq", 2, 0, 4
    )
    larger = jnp.max(pieces[1], axis=0)
    scales = jnp.exp(pieces[1] - larger[None])
    merged = jnp.sum(pieces[0] * scales[..., None], axis=0)
    summed = jnp.sum(pieces[2] * scales, axis=0)
    attention = merged / summed[..., None]
    attention = jnp.transpose(attention, (2, 0, 1, 3)).reshape(node_count, -1).astype(jnp.bfloat16)
    head_rows = collect(attention, "req", 0)
    projector = out_weight.reshape(-1, out_weight.shape[2])
    attended = sum_at_owner(
        jnp.dot(head_rows, projector, preferred_element_type=jnp.float32), ("seq", "side"), 0
    ).astype(jnp.bfloat16)
    local_experts = in_experts.shape[0]
    flat_ids = gate_experts.reshape(-1)
    expert_hit = (flat_ids[:, None] == jnp.arange(EXPERTS, dtype=jnp.int32)[None, :]).astype(
        jnp.int32
    )
    earlier = jnp.cumsum(expert_hit, axis=0) - expert_hit
    slot_rank = jnp.sum(earlier * expert_hit, axis=1)
    slot_ids = (flat_ids * CAP + slot_rank).reshape(gate_experts.shape)
    slot_count = EXPERTS * CAP
    matches = jnp.arange(slot_count, dtype=jnp.int32)[:, None, None] == slot_ids[None]
    placing = jnp.any(matches, axis=2).astype(jnp.bfloat16)
    mixing = jnp.sum(jnp.where(matches, gate_weights[None], 0.0), axis=2)
    outgoing = jnp.dot(placing, attended, preferred_element_type=jnp.float32).astype(jnp.bfloat16)
    device_count = EXPERTS // local_experts
    outgoing = outgoing.reshape(device_count, local_experts, CAP, -1)
    before = jnp.einsum(
        "sekd,edf->sekf",
        lax.all_to_all(outgoing, ("seq", "side"), split_axis=0, concat_axis=0, tiled=True),
        in_experts,
        preferred_element_type=jnp.float32,
    )
    hidden_part = sum_at_owner(before, "req", 3)
    hidden = collect(jax.nn.silu(hidden_part).astype(jnp.bfloat16), "req", 3)
    produced = jnp.einsum(
        "sekf,efd->sekd", hidden, out_experts, preferred_element_type=jnp.float32
    ).astype(jnp.bfloat16)
    came_back = lax.all_to_all(produced, ("seq", "side"), split_axis=0, concat_axis=0, tiled=True)
    slot_rows = came_back.reshape(slot_count, -1).astype(jnp.float32)
    expert_mix = jnp.dot(mixing.T, slot_rows, precision=lax.Precision.HIGHEST)
    return (attended, expert_mix.astype(jnp.bfloat16))


def solution(mesh):
    placed = (
        P(("groups", "req"), "seq", "side", None),
        P(("groups", "req"), "seq", "side"),
        P(("groups", "req"), "seq", "side"),
        P(("groups", "req"), "seq", "side"),
        P(("groups", "req"), "seq", "side"),
        P(("groups", "req"), None),
        P(("groups", "req")),
        P("side", "seq", "req"),
        P(("seq", "side"), "req", None),
        P(("seq", "side"), None, "req"),
        P(("groups", "seq", "side"), None),
        P(("groups", "seq", "side"), None),
    )
    return jax.shard_map(
        per_device,
        mesh=mesh,
        in_specs=placed,
        out_specs=(P(("groups", "seq", "side"), "req"), P(("groups", "seq", "side"), "req")),
        check_vma=False,
    )
```

profile of v0, /device:TPU:65, one launch (start us, length us, event | category | flops | bytes accessed | tf_op | source)
XLA Modules:
  0.0 484.4 jit_solution(6784699280962095466)
XLA Ops:
  0.6 0.0 copy-start
  0.6 1.0 copy.120
  1.7 1.1 broadcast_in_dim.68
  2.8 44.4 %all-to-all-start = ((bf16[16,1,8,2,2048]{4,2,3,1,0:T(8,128)(2,1)}), bf16[16,1,8,2,2048]{4,2,3,1,0:T(8,128)(2,1)S(1)}, u32[]{:S(2)}, u32[]{:S(2)}) async-start(bf16[16,1,8,2,2048]{4,2,3,1,0:T(8,128)(2,1)} %broadcast_in_dim.68), calls=%async_computation | async-start | bytes 2097152 | tf_op jit(solution)/shard_map/all_to_all | solution.py:25
  47.1 0.0 copy-start.7
  47.2 0.0 copy-start.4
  47.9 0.3 convolution_minimum_fusion.5
  48.3 0.2 convolution_minimum_fusion.4
  48.5 0.2 convolution_minimum_fusion.3
  48.7 0.2 convolution_minimum_fusion.2
  48.9 0.2 convolution_minimum_fusion.1
  49.1 0.2 convolution_minimum_fusion
  49.3 0.2 fusion.67
  49.6 0.1 pad_add_fusion
  49.7 41.8 %all-to-all-done = bf16[16,1,8,2,2048]{4,2,3,1,0:T(8,128)(2,1)S(1)} async-done(((bf16[16,1,8,2,2048]{4,2,3,1,0:T(8,128)(2,1)}), bf16[16,1,8,2,2048]{4,2,3,1,0:T(8,128)(2,1)S(1)}, u32[]{:S(2)}, u32[]{:S(2)}) %all-to-all-start) | async-done | bytes 1048608 | tf_op jit(solution)/shard_map/all_to_all | solution.py:25
  91.5 0.1 copy.173
  91.6 0.9 fusion.64
  92.5 0.3 copy.124
  92.8 1.3 copy.122
  94.1 0.3 fusion.66
  94.4 0.3 fusion.65
  94.7 0.4 fusion.18
  95.2 0.4 convolution_bitcast_fusion.1
  95.6 0.4 convolution_bitcast_fusion
  96.0 0.2 maximum_bitcast_fusion
  96.2 0.2 pad_maximum_fusion
  96.4 1.6 copy.126
  98.0 112.9 %all_to_all.53 = f32[1,2,16,128,130]{3,1,4,0,2:T(2,128)S(1)} all-to-all(f32[1,2,16,128,130]{3,1,4,0,2:T(2,128)S(1)} %copy.126), channel_id=1, replica_groups=mesh['groups'=2,'seq'=16,'side'=2,'req'=8] {'seq'}, dimensions={2} | all-to-all | bytes 4259840 | tf_op jit(solution)/shard_map/all_to_all | solution.py:36
  211.1 0.9 fusion
  212.0 0.1 copy.130
  212.1 20.8 %all_to_all.54 = bf16[8,128,256]{2,1,0:T(8,128)(2,1)S(1)} all-to-all(bf16[8,128,256]{2,1,0:T(8,128)(2,1)S(1)} %broadcast_in_dim.72), channel_id=1, replica_groups=mesh['groups'=2,'seq'=16,'side'=2,'req'=8] {'req'}, dimensions={0} | all-to-all | bytes 1048576 | tf_op jit(solution)/shard_map/all_to_all | solution.py:25
  232.9 1.7 fusion.68
  234.6 9.7 %all-to-all-start.3 = ((f32[32,32,512]{2,1,0:T(8,128)}), f32[32,32,512]{2,1,0:T(8,128)}, u32[]{:S(2)}, u32[]{:S(2)}) async-start(f32[32,32,512]{2,1,0:T(8,128)} %fusion.68), calls=%async_computation.3 | async-start | bytes 4194304 | tf_op jit(solution)/shard_map/all_to_all | solution.py:54
  244.4 0.1 copy.131
  244.5 0.1 eq.66
  244.5 0.1 eq.62
  244.7 0.6 reduce-window.6
  245.3 0.2 slice_reduce_fusion
  245.5 0.1 fusion.38
  245.6 0.1 reduce_sum.83
  245.7 0.2 fusion.33
  245.9 97.2 %all-to-all-done.3 = f32[32,32,512]{2,1,0:T(8,128)} async-done(((f32[32,32,512]{2,1,0:T(8,128)}), f32[32,32,512]{2,1,0:T(8,128)}, u32[]{:S(2)}, u32[]{:S(2)}) %all-to-all-start.3) | async-done | bytes 2097184 | tf_op jit(solution)/shard_map/all_to_all | solution.py:54
  343.1 1.8 reduce_sum.81
  344.9 0.0 copy-start.2
  344.9 0.3 convolution_convert_fusion
  345.2 0.1 reshape.120
  345.4 0.3 copy.136
  345.7 32.6 %all_to_all.55 = bf16[32,2,6,512]{3,1,2,0:T(2,128)(2,1)S(1)} all-to-all(bf16[32,2,6,512]{3,1,2,0:T(2,128)(2,1)S(1)} %copy.136), channel_id=1, replica_groups=mesh['groups'=2,'seq'=16,'side'=2,'req'=8] {'seq','side'}, dimensions={0} | all-to-all | bytes 786432 | tf_op jit(solution)/shard_map/all_to_all | solution.py:158
  378.3 0.6 fusion.5
  378.8 0.2 copy.172
  379.1 42.4 %all_to_all.56 = f32[8,32,2,6,128]{4,1,3,2,0:T(8,128)} all-to-all(f32[8,32,2,6,128]{4,1,3,2,0:T(8,128)S(1)} %bitcast.179), channel_id=1, replica_groups=mesh['groups'=2,'seq'=16,'side'=2,'req'=8] {'req'}, dimensions={0} | all-to-all | bytes 3145728 | tf_op jit(solution)/shard_map/all_to_all | solution.py:54
  421.4 1.6 reduce_sum.85
  423.0 0.1 multiply_convert_fusion
  423.1 0.1 broadcast_in_dim.75
  423.2 22.9 %all_to_all.57 = bf16[8,32,2,6,128]{4,1,3,2,0:T(8,128)(2,1)S(1)} all-to-all(bf16[8,32,2,6,128]{4,1,3,2,0:T(8,128)(2,1)S(1)} %broadcast_in_dim.75), channel_id=1, replica_groups=mesh['groups'=2,'seq'=16,'side'=2,'req'=8] {'req'}, dimensions={0} | all-to-all | bytes 1572864 | tf_op jit(solution)/shard_map/all_to_all | solution.py:25
  446.1 0.6 fusion.15
  446.7 1.1 copy.140
  447.8 7.6 %all-to-all-start.7 = ((bf16[32,2,6,512]{3,1,2,0:T(2,128)(2,1)}), bf16[32,2,6,512]{3,1,2,0:T(2,128)(2,1)S(1)}, u32[]{:S(2)}, u32[]{:S(2)}) async-start(bf16[32,2,6,512]{3,1,2,0:T(2,128)(2,1)} %copy.140), calls=%async_computation.7 | async-start | bytes 786432 | tf_op jit(solution)/shard_map/all_to_all | solution.py:167
  455.4 0.1 copy.135
  455.5 0.2 select_reduce_fusion
  455.7 27.6 %all-to-all-done.7 = bf16[32,2,6,512]{3,1,2,0:T(2,128)(2,1)S(1)} async-done(((bf16[32,2,6,512]{3,1,2,0:T(2,128)(2,1)}), bf16[32,2,6,512]{3,1,2,0:T(2,128)(2,1)S(1)}, u32[]{:S(2)}, u32[]{:S(2)}) %all-to-all-start.7) | async-done | bytes 393248 | tf_op jit(solution)/shard_map/all_to_all | solution.py:167
  483.2 0.1 copy.141
  483.3 0.1 reshape.123
  483.5 0.9 convolution_convert_fusion.1
  (36 shorter events, 0.3 us)
Async XLA Ops:
  0.6 377.6 %copy-start = (bf16[2,512,1024]{2,1,0:T(8,128)(2,1)S(1)}, bf16[2,512,1024]{2,1,0:T(8,128)(2,1)}, u32[]{:S(2)}) copy-start(bf16[2,512,1024]{2,1,0:T(8,128)(2,1)} %param.20) | copy-start | bytes 6291460
  2.8 45.1 %copy-start.10 = (s32[1,128]{1,0:T(1,128)S(1)}, s32[1,128]{1,0:T(1,128)}, u32[]{:S(2)}) copy-start(s32[1,128]{1,0:T(1,128)} %param.17) | copy-start | bytes 1540
  2.8 88.7 %all-to-all-start = ((bf16[16,1,8,2,2048]{4,2,3,1,0:T(8,128)(2,1)}), bf16[16,1,8,2,2048]{4,2,3,1,0:T(8,128)(2,1)S(1)}, u32[]{:S(2)}, u32[]{:S(2)}) async-start(bf16[16,1,8,2,2048]{4,2,3,1,0:T(8,128)(2,1)} %broadcast_in_dim.68), calls=%async_computation | async-start | bytes 2097152 | tf_op jit(solution)/shard_map/all_to_all | solution.py:25
  47.1 2.4 copy-start.7
  47.1 2.4 copy-start.8
  47.2 2.5 copy-start.3
  47.2 2.5 copy-start.4
  211.9 21.0 %copy-start.1 = (bf16[2,128,512]{2,1,0:T(8,128)(2,1)S(1)}, bf16[2,128,512]{2,1,0:T(8,128)(2,1)}, u32[]{:S(2)}) copy-start(bf16[2,128,512]{2,1,0:T(8,128)(2,1)} %param.19) | copy-start | bytes 786436
  234.6 9.7 %copy-start.5 = (s32[32,8]{0,1:T(8,128)S(1)}, s32[32,8]{0,1:T(8,128)}, u32[]{:S(2)}) copy-start(s32[32,8]{0,1:T(8,128)} %param.22) | copy-start | bytes 3076
  234.6 108.5 %all-to-all-start.3 = ((f32[32,32,512]{2,1,0:T(8,128)}), f32[32,32,512]{2,1,0:T(8,128)}, u32[]{:S(2)}, u32[]{:S(2)}) async-start(f32[32,32,512]{2,1,0:T(8,128)} %fusion.68), calls=%async_computation.3 | async-start | bytes 4194304 | tf_op jit(solution)/shard_map/all_to_all | solution.py:54
  344.9 0.8 copy-start.2
  423.1 23.0 %copy-start.9 = (bf16[2,1024,512]{2,1,0:T(8,128)(2,1)S(1)}, bf16[2,1024,512]{2,1,0:T(8,128)(2,1)}, u32[]{:S(2)}) copy-start(bf16[2,1024,512]{2,1,0:T(8,128)(2,1)} %param.21) | copy-start | bytes 6291460
  446.7 8.7 %copy-start.6 = (f32[32,8]{0,1:T(8,128)S(1)}, f32[32,8]{0,1:T(8,128)}, u32[]{:S(2)}) copy-start(f32[32,8]{0,1:T(8,128)} %param.23) | copy-start | bytes 3076
  447.8 35.4 %all-to-all-start.7 = ((bf16[32,2,6,512]{3,1,2,0:T(2,128)(2,1)}), bf16[32,2,6,512]{3,1,2,0:T(2,128)(2,1)S(1)}, u32[]{:S(2)}, u32[]{:S(2)}) async-start(bf16[32,2,6,512]{3,1,2,0:T(2,128)(2,1)} %copy.140), calls=%async_computation.7 | async-start | bytes 786432 | tf_op jit(solution)/shard_map/all_to_all | solution.py:167
where the time goes:
time: 485 us; the launch traced here: 484 us
  blocking collectives  232 us (48%)
  waiting for transfers between devices  167 us (34%)
  starting transfers between devices  61.6 us (13%)
  local copies, waits for them, and re-layouts  9.31 us (2%)
  matrix products  7.09 us (1%)
  other arithmetic  6.45 us (1%)
    all_to_all x1, blocking collectives, sent_together(): lax.all_to_all(both, axis, split_axis=split_dim, concat_axis=concat_dim,...  113 us
    all_to_all x1, waiting for transfers between devices, sum_at_owner(): blocks = lax.all_to_all(in_blocks(x, dim, count), axis, 0, 0, tiled=True)  97.2 us
    all_to_all x1, starting transfers between devices, sent_to_all(): return lax.all_to_all(copies, axis, split_axis=0, concat_axis=0, tiled=True)  44.4 us
    all_to_all x2, blocking collectives, sent_to_all(): return lax.all_to_all(copies, axis, split_axis=0, concat_axis=0, tiled=True)  43.6 us
    all_to_all x1, blocking collectives, sum_at_owner(): blocks = lax.all_to_all(in_blocks(x, dim, count), axis, 0, 0, tiled=True)  42.4 us
    all_to_all x1, waiting for transfers between devices, sent_to_all(): return lax.all_to_all(copies, axis, split_axis=0, concat_axis=0, tiled=True)  41.8 us
    all_to_all x1, blocking collectives, per_device(): lax.all_to_all(outgoing, ('seq', 'side'), split_axis=0, concat_axis=0, ti...  32.6 us
    all_to_all x1, waiting for transfers between devices, per_device(): lax.all_to_all(produced, ('seq', 'side'), split_axis=0, concat_axis=0, ti...  27.6 us
  transfers between devices with their start and end apart: 3, of which 3 were waited for; matrix products, arithmetic and copies ran while one was open for 1% of the time, Pallas kernels for 0%

commit v1 on v0

v1 whole, which is shorter than its diff:
```python
import functools
import math

import jax
import jax.numpy as jnp
from jax import lax
from jax.experimental import pallas as pl
from jax.experimental.pallas import tpu as pltpu
from jax.sharding import PartitionSpec as P

HD = 128
CAP = 6
NEG_FILL = -1e30
F32 = jnp.float32
BF16 = jnp.bfloat16
MESH = pl.DeviceIdType.MESH
MINUS, PLUS = 0, 1


def nt(a, b):
    return lax.dot_general(a, b, (((1,), (1,)), ((), ())), preferred_element_type=F32)


def nn(a, b):
    return lax.dot_general(a, b, (((1,), (0,)), ((), ())), preferred_element_type=F32)


def steps_of(n, j, way):
    short = (j + way) % 2
    return n // 2 - short


class Ring:
    def __init__(self, axis, n, me, send_sem, recv_sem, started):
        self.axis, self.n, self.me = axis, n, me
        self.send_sem, self.recv_sem, self.started = send_sem, recv_sem, started

    def at(self, offset):
        return lax.rem(self.me + (offset + self.n) % self.n, self.n)

    def copy(self, src, dst, j, way, s):
        return pltpu.make_async_remote_copy(
            src_ref=src,
            dst_ref=dst,
            send_sem=self.send_sem.at[j, way, s],
            recv_sem=self.recv_sem.at[j, way, s],
            device_id={self.axis: self.at(-1 if way == MINUS else 1)},
            device_id_type=MESH,
        )

    def send(self, src, dst, j, way, s):
        c = self.copy(src, dst, j, way, s)
        c.start()
        self.started.append(c)

    def arrived(self, ref, j, way, s):
        self.copy(ref, ref, j, way, s).wait_recv()


class Gather(Ring):
    def set(self, views):
        self.views = views
        return self

    def source(self, way, s):
        return self.at(s if way == MINUS else -s)

    def forward(self, j, way, s):
        if s < steps_of(self.n, j, way):
            ref = self.views[j](self.source(way, s))
            self.send(ref, ref, j, way, s)

    def begin(self, j):
        for way in (MINUS, PLUS):
            self.forward(j, way, 0)

    def take(self, j, way, s):
        if s > steps_of(self.n, j, way):
            return None
        p = self.source(way, s)
        self.arrived(self.views[j](p), j, way, s - 1)
        self.forward(j, way, s)
        return p


def kernel(
    cfg,
    q_hbm, k_hbm, v_hbm, t_hbm, gate_hbm, w_hbm, win_hbm, wout_hbm, par_ref, len_ref,
    att_out, exp_out,
    kv, gbuf, qbuf, qmat, wb, win, wout, reach_ref, m_ref, l_ref, acc_ref, att, abuf, part,
    rs_out, rs_in, xall, hit_ref, wsel_ref, pmat, pt, wrow, rows, hs_out, hs_in, hbuf, prod, sib_out, sib_in,
    rt_out, rt_in,
    load_sem, q_s, q_r, kv_s, kv_r, sib_s, sib_r, xa_s, xa_r, rs_s, rs_r, ag_s, ag_r, sx_s, sx_r,
    hr_s, hr_r, hg_s, hg_r, rt_s, rt_r,
):
    nz, nx, kvl, nl, tb, zpr, top, el, sl = cfg
    z, side, x = lax.axis_index("seq"), lax.axis_index("side"), lax.axis_index("req")
    other = 1 - side
    nodes = nz * nl
    sent = []

    loads = []

    def load(src, dst):
        c = pltpu.make_async_copy(src, dst, load_sem.at[len(loads)])
        c.start()
        loads.append(c)

    ctx = k_hbm.shape[0]
    tr = t_hbm.shape[0]
    load(q_hbm, qbuf.at[0])
    load(k_hbm, kv.at[z, pl.ds(0, ctx)])
    load(t_hbm, kv.at[z, pl.ds(ctx, tr)])
    load(v_hbm, kv.at[z, pl.ds(ctx + tr, ctx)])
    load(gate_hbm, gbuf.at[side, z])
    load(w_hbm, wb.at[side])
    load(win_hbm, win)
    load(wout_hbm, wout)

    barrier = pltpu.get_barrier_semaphore()
    peers = [{"seq": lax.rem(z + d, nz)} for d in range(1, nz)]
    peers += [{"req": lax.rem(x + d, nx)} for d in sorted({1, nx - 1})]
    peers += [{"side": other}]
    for peer in peers:
        pl.semaphore_signal(barrier, inc=1, device_id=peer, device_id_type=MESH)
    pl.semaphore_wait(barrier, len(peers))

    def sibling(src, dst, i):
        return pltpu.make_async_remote_copy(
            src_ref=src, dst_ref=dst, send_sem=sib_s.at[i], recv_sem=sib_r.at[i],
            device_id={"side": other}, device_id_type=MESH,
        )

    def sibling_send(src, dst, i):
        c = sibling(src, dst, i)
        c.start()
        sent.append(c)

    loads[0].wait()
    for d in range(1, nz):
        to = lax.rem(z + d, nz)
        c = pltpu.make_async_remote_copy(
            src_ref=qbuf.at[0, to], dst_ref=qbuf.at[1, z], send_sem=q_s.at[d - 1], recv_sem=q_r.at[d - 1],
            device_id={"seq": to}, device_id_type=MESH,
        )
        c.start()
        sent.append(c)
    views = [
        lambda p: kv.at[p, pl.ds(0, ctx + tr)],
        lambda p: kv.at[p, pl.ds(ctx + tr, ctx)],
        lambda p: gbuf.at[side, p],
    ]
    ring = Gather("seq", nz, z, kv_s, kv_r, sent).set(views)
    loads[1].wait()
    loads[2].wait()
    ring.begin(0)
    loads[3].wait()
    ring.begin(1)
    loads[4].wait()
    ring.begin(2)
    loads[5].wait()
    sibling_send(wb.at[side], wb.at[side], 0)

    row_i = lax.broadcasted_iota(jnp.int32, (nodes, nodes), 0)
    col_i = lax.broadcasted_iota(jnp.int32, (nodes, nodes), 1)
    eye = jnp.where(row_i == col_i, 1.0, 0.0)
    back = jnp.maximum(jnp.where(row_i == par_ref[...], 1.0, 0.0), eye)
    for turn in range(max(1, (nodes - 1).bit_length())):
        low = back.astype(BF16)
        back = jnp.minimum(nn(low, low), 1.0)
    reach = nt(eye.astype(BF16), back.astype(BF16)).astype(BF16)
    spread_row = lax.broadcasted_iota(jnp.int32, (nodes, nz * tr), 0)
    spread_col = lax.broadcasted_iota(jnp.int32, (nodes, nz * tr), 1)
    spread = jnp.where(spread_col == (spread_row // nl) * tr + lax.rem(spread_row, nl), 1.0, 0.0)
    reach_ref[...] = nn(reach, spread.astype(BF16))

    for d in range(1, nz):
        frm = lax.rem(z + nz - d, nz)
        pltpu.make_async_remote_copy(
            src_ref=qbuf.at[0, frm], dst_ref=qbuf.at[1, frm], send_sem=q_s.at[d - 1], recv_sem=q_r.at[d - 1],
            device_id={"seq": frm}, device_id_type=MESH,
        ).wait_recv()
    qbuf[1, z] = qbuf[0, z]
    q_all = qbuf[1].astype(F32).reshape(nz, kvl, nl, HD)
    for c in range(kvl):
        qmat[c] = q_all[:, c].reshape(nodes, HD).astype(BF16)
    factor = 1.0 / math.sqrt(HD)
    m_ref[...] = jnp.full_like(m_ref, NEG_FILL)
    l_ref[...] = jnp.zeros_like(l_ref)
    acc_ref[...] = jnp.zeros_like(acc_ref)

    def absorb(c, keys, seen, values, shift):
        scores = jnp.where(seen, nt(qmat[c], keys) * factor, NEG_FILL)
        old = m_ref[c]
        new = jnp.maximum(old, jnp.max(scores, axis=1, keepdims=True))
        weights = jnp.where(seen, jnp.exp(scores - new), 0.0)
        scale = jnp.exp(old - new)
        m_ref[c] = new
        l_ref[c] = l_ref[c] * scale + jnp.sum(weights, axis=1, keepdims=True)
        if shift:
            weights = pltpu.roll(weights, shift, 1)
        acc_ref[c] = acc_ref[c] * scale + nn(weights.astype(BF16), values)

    length = len_ref[0]
    key_pos = lax.broadcasted_iota(jnp.int32, (nodes, ctx), 1)

    def attend(p):
        seen = key_pos + p * ctx < length
        for c in range(kvl):
            lanes = slice(c * HD, (c + 1) * HD)
            absorb(c, kv[p, 0:ctx, lanes], seen, kv[p, ctx + tr : 2 * ctx + tr, lanes], 0)

    attend(z)
    for s in range(1, nz // 2 + 1):
        got = [[ring.take(j, way, s) for j in range(3)] for way in (MINUS, PLUS)]
        if s < nz // 2:
            attend(got[MINUS][0])
            attend(got[PLUS][0])
        else:
            attend(got[MINUS][0])
    sibling_send(gbuf.at[side], gbuf.at[side], 1)

    for c in range(kvl):
        lanes = slice(c * HD, (c + 1) * HD)
        tree = kv[:, ctx : ctx + tr, lanes].reshape(nz * tr, HD)
        absorb(c, tree, reach_ref[...] > 0.5, tree, nl)
        att[:, :, lanes] = (acc_ref[c] / l_ref[c]).astype(BF16).reshape(zpr * 2, tb, HD)

    for h in range(zpr):
        sibling_send(att.at[2 * h + other], abuf.at[x, side, h], 2 + h)
    for h in range(zpr):
        abuf[x, side, h] = att[2 * h + side]
    ring = Gather("req", nx, x, xa_s, xa_r, sent).set([lambda p: abuf.at[p, side], lambda p: abuf.at[p, other]])
    ring.begin(0)
    for h in range(zpr):
        sibling(att.at[2 * h + other], abuf.at[x, other, h], 2 + h).wait_recv()
    ring.begin(1)
    sibling(wb.at[side], wb.at[other], 0).wait_recv()

    def project(r):
        a0 = abuf[r, 0].reshape(zpr * tb, kvl * HD)
        a1 = abuf[r, 1].reshape(zpr * tb, kvl * HD)
        part[pl.ds(r * zpr, zpr)] = (nn(a0, wb[0]) + nn(a1, wb[1])).reshape(zpr, tb, -1)

    project(x)
    for s in range(1, nx // 2 + 1):
        got = [[ring.take(j, way, s) for j in range(2)] for way in (MINUS, PLUS)]
        if s < nx // 2:
            project(got[MINUS][0])
            project(got[PLUS][0])
        else:
            project(got[MINUS][0])

    def reduce_scatter(ring, out, inn, own, chunks):
        n = ring.n

        def put(j, way, s):
            steps = steps_of(n, j, way)
            if s >= steps:
                return
            left = steps - s
            value = own(ring.at(-left if way == MINUS else left), j)
            if s > 0:
                ring.arrived(inn.at[j, way, s - 1], j, way, s - 1)
                value = value + inn[j, way, s - 1].astype(F32)
            out[j, way, s] = value.astype(BF16)
            ring.send(out.at[j, way, s], inn.at[j, way, s], j, way, s)

        for s in range(n // 2):
            for j in range(chunks):
                for way in (MINUS, PLUS):
                    put(j, way, s)

        def total(j):
            value = own(ring.me, j)
            for way in (MINUS, PLUS):
                steps = steps_of(n, j, way)
                if steps:
                    ring.arrived(inn.at[j, way, steps - 1], j, way, steps - 1)
                    value = value + inn[j, way, steps - 1].astype(F32)
            return value

        return total

    half = tb // 2
    ring = Ring("seq", nz, z, rs_s, rs_r, sent)
    total = reduce_scatter(ring, rs_out, rs_in, lambda p, j: part[p, pl.ds(j * half, half), :], 2)
    ring = Gather("seq", nz, z, ag_s, ag_r, sent).set(
        [functools.partial(lambda j, p: xall.at[p, side, pl.ds(j * half, half)], j) for j in range(2)]
    )

    def across(j, way, s, p, whose):
        ref = xall.at[p, whose, pl.ds(j * half, half)]
        return pltpu.make_async_remote_copy(
            src_ref=ref, dst_ref=ref, send_sem=sx_s.at[j, way, s], recv_sem=sx_r.at[j, way, s],
            device_id={"side": other}, device_id_type=MESH,
        )

    def hand_over(j, way, s, p):
        c = across(j, way, s, p, side)
        c.start()
        sent.append(c)

    for j in range(2):
        xall[z, side, pl.ds(j * half, half)] = total(j).astype(BF16)
        ring.begin(j)
        hand_over(j, MINUS, 0, z)
    att_out[...] = xall[z, side]

    sibling(gbuf.at[side], gbuf.at[other], 1).wait_recv()
    upper = jnp.where(row_i <= col_i, 1.0, 0.0).astype(BF16)
    slot_i = lax.broadcasted_iota(jnp.int32, (sl, nodes), 0).astype(F32)
    first = ((z * 2 + side) * el + 1).astype(F32)
    for r in range(nx):
        gates = jnp.zeros((2 * top, nodes), F32)
        for h in range(zpr):
            for w in range(2):
                gates = gates + gbuf[w, r * zpr + h].astype(F32)
        for e in range(el):
            match = jnp.where(gates[:top] == first + e, 1.0, 0.0)
            hit_ref[e, r : r + 1] = jnp.sum(match, axis=0, keepdims=True)
            wsel_ref[e, r : r + 1] = jnp.sum(match * gates[top:], axis=0, keepdims=True)
    for e in range(el):
        hits = hit_ref[e]
        ranks = nn(hits.astype(BF16), upper)
        before = jnp.zeros((1, 1), F32)
        total_w = jnp.zeros((sl, 1), F32)
        for r in range(nx):
            slot = jnp.where(hits[r : r + 1] > 0.5, ranks[r : r + 1] + before - 1.0, -1.0)
            place = jnp.where(slot_i == slot, 1.0, 0.0)
            total_w = total_w + jnp.sum(place * wsel_ref[e, r : r + 1], axis=1, keepdims=True)
            pmat[pl.ds(e * sl, sl), r * nodes : (r + 1) * nodes] = place.astype(BF16)
            before = before + ranks[r : r + 1, nodes - 1 :]
        wrow[pl.ds(e * sl, sl)] = total_w
    eye_low = eye.astype(BF16)
    for r in range(nx):
        pt[pl.ds(r * nodes, nodes)] = nt(eye_low, pmat[:, r * nodes : (r + 1) * nodes]).astype(BF16)

    for s in range(1, nz // 2 + 1):
        for j in range(2):
            for way in (MINUS, PLUS):
                p = ring.take(j, way, s)
                if p is not None:
                    hand_over(j, way, s, p)
    for s in range(nz // 2 + 1):
        for j in range(2):
            for way in (MINUS, PLUS):
                if s <= steps_of(nz, j, way) and (s or way == MINUS):
                    across(j, way, s, ring.source(way, s), other).wait_recv()

    tokens = nz * 2 * tb
    flat = xall[...].reshape(tokens, xall.shape[-1])
    for e in range(el):
        rows[e] = nn(pmat[pl.ds(e * sl, sl)], flat).astype(BF16)
    loads[6].wait()
    hb = hbuf.shape[-1]
    ring = Ring("req", nx, x, hr_s, hr_r, sent)
    total = reduce_scatter(
        ring, hs_out, hs_in,
        lambda p, e: nn(rows[e], win[e, :, pl.ds(pl.multiple_of(p * hb, hb), hb)]), el,
    )
    ring = Gather("req", nx, x, hg_s, hg_r, sent).set(
        [functools.partial(lambda e, p: hbuf.at[p, e], e) for e in range(el)]
    )
    for e in range(el):
        value = total(e)
        hbuf[x, e] = (value / (1.0 + jnp.exp(-value))).astype(BF16)
        ring.begin(e)
    loads[7].wait()

    def produce(p, e):
        return nn(hbuf[p, e], wout[e, pl.ds(pl.multiple_of(p * hb, hb), hb), :])

    for e in range(el):
        prod[e] = produce(x, e)
    for s in range(1, nx // 2 + 1):
        for e in range(el):
            for way in (MINUS, PLUS):
                p = ring.take(e, way, s)
                if p is not None:
                    prod[e] = prod[e] + produce(p, e)
    for e in range(el):
        rows[e] = (prod[e] * wrow[pl.ds(e * sl, sl)]).astype(BF16)
    made = rows[...].reshape(el * sl, -1)
    for r in range(nx):
        mixed = nn(pt[pl.ds(r * nodes, nodes)], made).reshape(zpr, 2, tb, -1)
        for h in range(zpr):
            for w in range(2):
                @pl.when(side == w)
                def _():
                    part[r * zpr + h] = mixed[h, w]

                @pl.when(side != w)
                def _():
                    sib_out[r * zpr + h] = mixed[h, w].astype(BF16)
    sibling_send(sib_out, sib_in, 2 + zpr)
    sibling(sib_out, sib_in, 2 + zpr).wait_recv()
    ring = Ring("seq", nz, z, rt_s, rt_r, sent)
    total = reduce_scatter(
        ring, rt_out, rt_in,
        lambda p, j: part[p, pl.ds(j * half, half), :] + sib_in[p, pl.ds(j * half, half), :].astype(F32), 2,
    )
    for j in range(2):
        exp_out[pl.ds(j * half, half)] = total(j).astype(BF16)
    for c in sent:
        c.wait_send()


def per_device(
    queries, cache_keys, cache_values, tree_keys, tree_values, parents, lengths,
    out_weight, in_experts, out_experts, gate_experts, gate_weights,
):
    nz, nx = lax.axis_size("seq"), lax.axis_size("req")
    sides = lax.axis_size("side")
    _, nl, kvl, gd = queries.shape
    ctx, width = cache_keys.shape[1], cache_keys.shape[2]
    tb, top = gate_experts.shape
    el, feats, ff = in_experts.shape
    zpr = nz // nx
    nodes = nz * nl
    sl = nz * sides * CAP
    hb = ff // nx
    half = tb // 2
    cols = out_weight.shape[2]

    q = queries[0].reshape(nl, kvl, nz, HD).transpose(2, 1, 0, 3).reshape(nz, kvl * nl, HD)
    tree = jnp.concatenate([tree_keys[0], tree_values[0]], axis=0)
    place = lax.rem(lax.axis_index("seq") * sides + lax.axis_index("side"), zpr * sides)
    both = jnp.concatenate([(gate_experts + 1).astype(F32), gate_weights], axis=1).T
    lane = jnp.arange(nodes, dtype=jnp.int32)[None, :]
    gates = jnp.where(lane // tb == place, jnp.tile(both, (1, zpr * sides)), 0.0).astype(BF16)
    wide = out_weight.reshape(kvl * HD, cols)

    cfg = (nz, nx, kvl, nl, tb, zpr, top, el, sl)
    any_spec = pl.BlockSpec(memory_space=pl.ANY)
    vmem_spec = pl.BlockSpec(memory_space=pltpu.VMEM)
    hz, hx = nz // 2, nx // 2
    dma = pltpu.SemaphoreType.DMA
    V = pltpu.VMEM
    tr = 2 * nl
    scratch = [
        V((nz, 2 * ctx + tr, width), BF16),
        V((2, nz, 2 * top, nodes), BF16),
        V((2, nz, kvl * nl, HD), BF16),
        V((kvl, nodes, HD), BF16),
        V((2, kvl * HD, cols), BF16),
        V((el, feats, ff), BF16),
        V((el, ff, cols), BF16),
        V((nodes, nz * tr), F32),
        V((kvl, nodes, 1), F32),
        V((kvl, nodes, 1), F32),
        V((kvl, nodes, HD), F32),
        V((zpr * 2, tb, kvl * HD), BF16),
        V((nx, 2, zpr, tb, kvl * HD), BF16),
        V((nz, tb, cols), F32),
        V((2, 2, hz, half, cols), BF16),
        V((2, 2, hz, half, cols), BF16),
        V((nz, 2, tb, cols), BF16),
        V((el, nx, nodes), F32),
        V((el, nx, nodes), F32),
        V((el * sl, nx * nodes), BF16),
        V((nx * nodes, el * sl), BF16),
        V((el * sl, 1), F32),
        V((el, sl, cols), BF16),
        V((el, 2, hx, sl, hb), BF16),
        V((el, 2, hx, sl, hb), BF16),
        V((nx, el, sl, hb), BF16),
        V((el, sl, cols), F32),
        V((nz, tb, cols), BF16),
        V((nz, tb, cols), BF16),
        V((2, 2, hz, half, cols), BF16),
        V((2, 2, hz, half, cols), BF16),
        dma((8,)),
        dma((nz - 1,)), dma((nz - 1,)),
        dma((3, 2, hz)), dma((3, 2, hz)),
        dma((3 + zpr,)), dma((3 + zpr,)),
        dma((2, 2, hx)), dma((2, 2, hx)),
        dma((2, 2, hz)), dma((2, 2, hz)),
        dma((2, 2, hz)), dma((2, 2, hz)),
        dma((2, 2, hz + 1)), dma((2, 2, hz + 1)),
        dma((el, 2, hx)), dma((el, 2, hx)),
        dma((el, 2, hx)), dma((el, 2, hx)),
        dma((2, 2, hz)), dma((2, 2, hz)),
    ]
    block = jax.ShapeDtypeStruct((tb, cols), BF16)
    return pl.pallas_call(
        functools.partial(kernel, cfg),
        out_shape=(block, block),
        in_specs=[any_spec] * 8 + [vmem_spec, pl.BlockSpec(memory_space=pltpu.SMEM)],
        out_specs=(vmem_spec, vmem_spec),
        scratch_shapes=scratch,
        compiler_params=pltpu.CompilerParams(
            collective_id=0, has_side_effects=True, vmem_limit_bytes=48 * 1024 * 1024
        ),
    )(q, cache_keys[0], cache_values[0], tree, gates, wide, in_experts, out_experts, parents, lengths)


def solution(mesh):
    placed = (
        P(("groups", "req"), "seq", "side", None),
        P(("groups", "req"), "seq", "side"),
        P(("groups", "req"), "seq", "side"),
        P(("groups", "req"), "seq", "side"),
        P(("groups", "req"), "seq", "side"),
        P(("groups", "req"), None),
        P(("groups", "req")),
        P("side", "seq", "req"),
        P(("seq", "side"), "req", None),
        P(("seq", "side"), None, "req"),
        P(("groups", "seq", "side"), None),
        P(("groups", "seq", "side"), None),
    )
    return jax.shard_map(
        per_device,
        mesh=mesh,
        in_specs=placed,
        out_specs=(P(("groups", "seq", "side"), "req"), P(("groups", "seq", "side"), "req")),
        check_vma=False,
    )
```

time: 485 us -> 230 us (0.47)
  blocking collectives: 232 us -> 0 us
  Pallas kernels: 0 us -> 214 us
  waiting for transfers between devices: 167 us -> 0 us
  starting transfers between devices: 61.6 us -> 0 us
  matrix products: 7.09 us -> 0 us
    all_to_all x5 -> x0, blocking collectives: 232 us -> none  [the longest x1 113 us: sent_together(): lax.all_to_all(both, axis, split_axis=split_dim, concat_axis=concat_dim,...]
    pallas_call x0 -> x1, Pallas kernels: none -> 214 us  [per_device(): pl.pallas_call(functools.partial(kernel, cfg), out_shape=(block, block),...]
    all_to_all x3 -> x0, waiting for transfers between devices: 167 us -> none  [the longest x1 97.2 us: sum_at_owner(): blocks = lax.all_to_all(in_blocks(x, dim, count), axis, 0, 0, tiled=True)]
    all_to_all x3 -> x0, starting transfers between devices: 61.6 us -> none  [the longest x1 44.4 us: sent_to_all(): return lax.all_to_all(copies, axis, split_axis=0, concat_axis=0, tiled=True)]
    unnamed x24 -> x14, local copies, waits for them, and re-layouts: 0.22 us -> 7.69 us
    dot_general x16 -> x0, matrix products: 7.09 us -> none  [the longest x1 1.73 us: per_device(): jnp.dot(head_rows, projector, preferred_element_type=jnp.float32)]
    reduce_sum x7 -> x0, other arithmetic: 4.96 us -> none  [the longest x2 3.32 us: sum_at_owner(): return jnp.sum(blocks, axis=0)]
  transfers between devices with their start and end apart: 3 -> 0, of which waited for: 3 -> 0; matrix products, arithmetic and copies ran while one was open for 1% -> 0% of each run, Pallas kernels for 0% -> 0%
where the time goes in v1:
time: 230 us; the launch traced here: 226 us
  Pallas kernels  214 us (93%)
  local copies, waits for them, and re-layouts  8.7 us (4%)
    pallas_call x1, Pallas kernels, per_device(): pl.pallas_call(functools.partial(kernel, cfg), out_shape=(block, block),...  214 us
    unnamed x14, local copies, waits for them, and re-layouts  7.69 us

profile of v1, /device:TPU:65, one launch (start us, length us, event | category | flops | bytes accessed | tf_op | source)
XLA Modules:
  0.0 226.1 jit_solution(14925621306184767234)
XLA Ops:
  1.3 0.7 add_convert_fusion
  2.0 0.7 maximum_bitcast_fusion
  2.7 0.7 pad_maximum_fusion.t_hbm
  3.4 0.1 tile.10
  3.5 0.9 reshape_squeeze.3
  4.4 0.0 copy-start
  4.4 1.6 copy-done
  6.0 0.0 copy-start.1
  6.0 1.6 copy-done.1
  7.6 0.0 copy-start.2
  7.6 0.9 copy-done.2
  8.6 0.0 copy-start.3
  8.6 0.8 copy-done.3
  9.4 0.0 copy-start.4
  9.4 0.8 copy-done.4
  10.2 0.0 copy-start.5
  10.2 0.7 copy-done.5
  10.9 214.0 %shard_map.131 = (bf16[32,512]{1,0:T(8,128)(2,1)S(1)}, bf16[32,512]{1,0:T(8,128)(2,1)S(1)}) custom-call(bf16[16,16,128]{2,1,0:T(8,128)(2,1)S(1)} %bitcast.12, bf16[128,256]{1,0:T(8,128)(2,1)S(1)} %bitcast.14, bf16[128,256]{1,0:T(8,128)(2,1)S(1)} %bitcast.15, bf16[16,256]{1,0:T(8,128)(2,1)S(1)} %pad_maximum_fusion.t_hbm, ...), custom_call_target="tpu_custom_call" | custom-call | tf_op jit(solution)/shard_map/pallas_call | solution.py:486
  224.9 0.6 copy.20
  225.5 0.6 copy.21
  (4 shorter events, 0.1 us)
Async XLA Ops:
  4.4 1.6 copy-start
  6.0 1.6 copy-start.1
  7.6 0.9 copy-start.2
  8.6 0.8 copy-start.3
  9.4 0.8 copy-start.4
  10.2 0.7 copy-start.5
